TPU v7x, 32 devices: a whole 2x2x4 slice. The times are simulated.
32 devices in a mesh: ctx: 8 (over z, y), tile: 4 (over x, core).
Axes of the slice: x: 2, y: 2, z: 4, core: 2. Of those that a mesh axis runs over, the one named last changes fastest.
Arguments:
- masks: bfloat16 [16, 512, 512], P('ctx', 'tile'), may hold values from 0 to 1
- blur_rows: bfloat16 [512, 512], replicated, may hold values from -0.25 to 0.25
- blur_cols: bfloat16 [512, 512], replicated, may hold values from -0.25 to 0.25
- pupils: float32 [6, 64, 128], replicated, may hold values from -5 to 5
- targets: bfloat16 [16, 512, 512], P('ctx', 'tile'), may hold values from 0 to 1
- context_masters: int32 [16, 12], P('ctx'), may hold values from 0 to 15, as said below
- offsets: int32 [16, 12, 2], P('ctx'), may hold values from 0 to 511
Outputs:
- resist: bfloat16 [16, 512, 512], P('ctx', 'tile')
- mask_grad: float32 [16, 512, 512], P('ctx', 'tile')
Inputs may be any that keep to these rules, and one draw needn't show every extreme that they name: `context_masters`: master m lies on ctx index m // 2. Among the masters named by the 2 contexts of one ctx index there is at most one lying on any one ctx index; a master may be named several times.
All inputs are finite; a program needn't handle non-finite values.
Results may differ from a plain program's by a relative error of at most 0.019.
Values may be sent and summed in bfloat16 or wider, within the bound.
No kernel may reach another device: no remote copies, remote signals or barrier semaphores. Data moves between devices by JAX's collectives and lax.ppermute only.
A program may use at most 64 MiB of HBM per device.

v0:
```python
import math
import jax
import jax.numpy as jnp
from jax import lax
from jax.sharding import PartitionSpec as P

STEEPNESS = 4.0
THRESHOLD = 1.0


def build_tables(extent, mode_count):
    frequency = (jnp.arange(mode_count, dtype=jnp.int32) - mode_count // 2) % extent
    positions = jnp.arange(extent, dtype=jnp.int32)
    windings = frequency[:, None] * positions[None, :] % extent
    angles = windings.astype(jnp.float32) * (2.0 * math.pi / extent)
    scale_factor = 1.0 / math.sqrt(extent)
    cosine_table = jnp.cos(angles) * scale_factor
    sine_table = jnp.sin(angles) * scale_factor
    row_real = cosine_table.astype(jnp.bfloat16)
    row_imag = (-sine_table).astype(jnp.bfloat16)
    col_fwd = jnp.concatenate([cosine_table.T, -sine_table.T], axis=1).astype(jnp.bfloat16)
    inverse_big = jnp.concatenate(
        [
            jnp.concatenate([cosine_table, sine_table], axis=1),
            jnp.concatenate([-sine_table, cosine_table], axis=1),
        ],
        axis=0,
    ).astype(jnp.bfloat16)
    back_real = cosine_table.T.astype(jnp.bfloat16)
    back_imag = sine_table.T.astype(jnp.bfloat16)
    adjoint_big = jnp.concatenate(
        [
            jnp.concatenate([cosine_table.T, -sine_table.T], axis=1),
            jnp.concatenate([sine_table.T, cosine_table.T], axis=1),
        ],
        axis=0,
    ).astype(jnp.bfloat16)
    return (row_real, row_imag, col_fwd, inverse_big, back_real, back_imag, adjoint_big)


def complex_left(left_real, left_imag, values):
    width = values.shape[-1] // 2
    real_lead = jnp.einsum("ux,...xv->...uv", left_real, values, preferred_element_type=jnp.float32)
    imag_lead = jnp.einsum("ux,...xv->...uv", left_imag, values, preferred_element_type=jnp.float32)
    return jnp.concatenate(
        [
            real_lead[..., :width] - imag_lead[..., width:],
            real_lead[..., width:] + imag_lead[..., :width],
        ],
        axis=-1,
    )


def complex_times(factor, values, conjugate):
    width = values.shape[-1] // 2
    factor_real = factor[..., :width]
    factor_imag = factor[..., width:]
    if conjugate:
        factor_imag = -factor_imag
    values_real = values[..., :width]
    values_imag = values[..., width:]
    return jnp.concatenate(
        [
            factor_real * values_real - factor_imag * values_imag,
            factor_real * values_imag + factor_imag * values_real,
        ],
        axis=-1,
    )


def phase_table(shifts, row_begin, band_rows, mode_count, extent):
    freq_u = (jnp.arange(band_rows, dtype=jnp.int32) + row_begin - mode_count // 2) % extent
    freq_v = (jnp.arange(mode_count, dtype=jnp.int32) - mode_count // 2) % extent
    windings = (
        freq_u[None, :, None] * shifts[:, 0][:, None, None]
        + freq_v[None, None, :] * shifts[:, 1][:, None, None]
    ) % extent
    angles = windings.astype(jnp.float32) * (2.0 * math.pi / extent)
    return jnp.concatenate([jnp.cos(angles), -jnp.sin(angles)], axis=-1)


def image_adjoint(
    spectrum, target, pupils, back_real, back_imag, row_real, row_imag, inverse_big, adjoint_big
):
    amplitude = complex_times(pupils, spectrum[None], False).astype(jnp.bfloat16)
    spread = jnp.einsum(
        "kuv,vy->kuy", amplitude, inverse_big, preferred_element_type=jnp.float32
    ).astype(jnp.bfloat16)
    field = complex_left(back_real, back_imag, spread)
    width = field.shape[-1] // 2
    field_real = field[..., :width]
    field_imag = field[..., width:]
    intensity = jnp.sum(field_real * field_real + field_imag * field_imag, axis=0)
    resist = jax.nn.sigmoid(STEEPNESS * (intensity - THRESHOLD))
    slope_term = (resist - target.astype(jnp.float32)) * STEEPNESS * resist * (1.0 - resist)
    pull_back = jnp.concatenate(
        [2.0 * slope_term * field_real, 2.0 * slope_term * field_imag], axis=-1
    ).astype(jnp.bfloat16)
    folded = jnp.einsum(
        "kxy,yv->kxv", pull_back, adjoint_big, preferred_element_type=jnp.float32
    ).astype(jnp.bfloat16)
    grad_amp = complex_left(row_real, row_imag, folded)
    grad_spec = jnp.sum(complex_times(pupils, grad_amp, True), axis=0)
    return (resist.astype(jnp.bfloat16), grad_spec)


def local(masks, blur_rows, blur_cols, pupils, targets, context_masters, offsets):
    ctx_count = lax.axis_size("ctx")
    owned, row_count, extent = masks.shape
    mode_count = pupils.shape[1]
    context_count = context_masters.shape[0]
    source_count = context_masters.shape[1]
    tile_pos = lax.axis_index("tile")
    row_start = tile_pos * row_count
    row_real, row_imag, col_fwd, inverse_big, back_real, back_imag, adjoint_big = build_tables(
        extent, mode_count
    )
    own_row_real = lax.dynamic_slice_in_dim(row_real, row_start, row_count, 1)
    own_row_imag = lax.dynamic_slice_in_dim(row_imag, row_start, row_count, 1)
    own_back_real = lax.dynamic_slice_in_dim(back_real, row_start, row_count, 0)
    own_back_imag = lax.dynamic_slice_in_dim(back_imag, row_start, row_count, 0)
    own_blur = lax.dynamic_slice_in_dim(blur_rows, row_start, row_count, 0)
    own_blur_cols = lax.dynamic_slice_in_dim(blur_rows, row_start, row_count, 1)
    owners = (context_masters // owned).reshape(-1)
    local_index = (context_masters % owned).reshape(-1)
    slot_index = jnp.arange(ctx_count, dtype=jnp.int32)
    owner_match = owners[:, None] == slot_index[None, :]
    wanted = jnp.max(jnp.where(owner_match, local_index[:, None] + 1, 0), axis=0)
    asked_for = lax.all_to_all(wanted[:, None], "ctx", split_axis=0, concat_axis=0, tiled=True)[
        :, 0
    ]
    chosen = asked_for[:, None] == jnp.arange(owned, dtype=jnp.int32)[None, :] + 1
    half_blur = jnp.einsum(
        "mxy,zy->mxz", masks, blur_cols, preferred_element_type=jnp.float32
    ).astype(jnp.bfloat16)
    weights = own_blur
    blurred = jnp.einsum(
        "xj,mjz->mxz",
        weights,
        lax.all_gather(half_blur, "tile", axis=1, tiled=True),
        preferred_element_type=jnp.float32,
    ).astype(jnp.bfloat16)
    column = jnp.einsum("mxy,yv->mxv", blurred, col_fwd, preferred_element_type=jnp.float32).astype(
        jnp.bfloat16
    )
    partial_value = complex_left(own_row_real, own_row_imag, column)
    spectra = lax.psum(partial_value.astype(jnp.bfloat16), "tile")
    outgoing = jnp.einsum(
        "dm,muv->duv", chosen.astype(jnp.bfloat16), spectra, preferred_element_type=jnp.float32
    ).astype(jnp.bfloat16)
    incoming = lax.all_to_all(outgoing, "ctx", split_axis=0, concat_axis=0, tiled=True)
    flat_shift = offsets.reshape(-1, 2)
    picked = jnp.take(incoming, owners, axis=0).astype(jnp.float32)
    turned = complex_times(
        phase_table(flat_shift, 0, mode_count, mode_count, extent), picked, False
    )
    context_spec = jnp.sum(
        turned.reshape(context_count, source_count, mode_count, 2 * mode_count), axis=1
    )

    def one_context(inputs):
        spectrum, target = inputs
        return image_adjoint(
            spectrum,
            target,
            pupils,
            own_back_real,
            own_back_imag,
            own_row_real,
            own_row_imag,
            inverse_big,
            adjoint_big,
        )

    resist, grad_part = lax.map(one_context, (context_spec, targets))
    grad_ctx = lax.psum(grad_part.astype(jnp.bfloat16), "tile").astype(jnp.float32)
    band_start = 0
    repeated = jnp.repeat(grad_ctx, source_count, axis=0)
    back_turn = complex_times(
        phase_table(flat_shift, band_start, mode_count, mode_count, extent), repeated, True
    )
    returned = jnp.einsum(
        "rd,ruv->duv", owner_match.astype(jnp.float32), back_turn, precision=lax.Precision.HIGHEST
    )
    arrived = lax.all_to_all(
        returned.astype(jnp.bfloat16), "ctx", split_axis=0, concat_axis=0, tiled=True
    ).astype(returned.dtype)
    master_grad = jnp.einsum(
        "dm,duv->muv", chosen.astype(jnp.float32), arrived, precision=lax.Precision.HIGHEST
    ).astype(jnp.bfloat16)
    lifted = jnp.einsum(
        "muv,vy->muy", master_grad, inverse_big, preferred_element_type=jnp.float32
    ).astype(jnp.bfloat16)
    surface = (
        jnp.einsum(
            "xu,muy->mxy", own_back_real, lifted[..., :extent], preferred_element_type=jnp.float32
        )
        - jnp.einsum(
            "xu,muy->mxy", own_back_imag, lifted[..., extent:], preferred_element_type=jnp.float32
        )
    ).astype(jnp.bfloat16)
    settled = jnp.einsum(
        "mxy,yz->mxz", surface, blur_cols, preferred_element_type=jnp.float32
    ).astype(jnp.bfloat16)
    weights = own_blur_cols
    mask_grad = jnp.einsum(
        "jx,mjz->mxz",
        weights,
        lax.all_gather(settled, "tile", axis=1, tiled=True),
        preferred_element_type=jnp.float32,
    )
    return (resist, mask_grad)


def solution(mesh):
    placed = (
        P("ctx", "tile", None),
        P(),
        P(),
        P(),
        P("ctx", "tile", None),
        P("ctx", None),
        P("ctx", None, None),
    )
    return jax.shard_map(
        local,
        mesh=mesh,
        in_specs=placed,
        out_specs=(P("ctx", "tile", None), P("ctx", "tile", None)),
        check_vma=False,
    )
```

profile of v0, /device:TPU:0, one launch (start us, length us, event | category | flops | bytes accessed | tf_op | source)
XLA Modules:
  0.0 133.8 jit_solution(16642103256916884030)
XLA Ops:
  7.2 1.0 copy-done
  8.2 2.0 %convolution_convert_fusion.4 = bf16[2,128,512]{2,1,0:T(8,128)(2,1)} fusion(bf16[2,128,512]{2,1,0:T(8,128)(2,1)} %param.9, bf16[512,512]{1,0:T(8,128)(2,1)S(1)} %copy-done), kind=kOutput, calls=%fused_computation.57 | convolution fusion | flops 134348800 | bytes 1048576 | tf_op jit(solution)/shard_map/mxy,zy->mxz/dot_general | solution.py:133
  10.2 0.7 and_select_fusion.1
  11.3 0.7 copy.75
  11.9 7.3 %all-to-all-start = ((s32[8,1,1]{2,1,0:T(1,128)}), s32[8,1,1]{2,1,0:T(1,128)S(1)}, u32[]{:S(2)}, u32[]{:S(2)}) async-start(s32[8,1,1]{2,1,0:T(1,128)} %copy.75), calls=%async_computation | async-start | bytes 8192 | tf_op jit(solution)/shard_map/all_to_all | solution.py:129
  19.3 0.7 copy.73
  20.1 1.1 fusion.45
  21.6 0.6 fusion.65
  22.2 1.1 cosine_multiply_fusion
  23.7 2.0 %all-to-all-done = s32[8,1,1]{2,1,0:T(1,128)S(1)} async-done(((s32[8,1,1]{2,1,0:T(1,128)}), s32[8,1,1]{2,1,0:T(1,128)S(1)}, u32[]{:S(2)}, u32[]{:S(2)}) %all-to-all-start) | async-done | bytes 64 | tf_op jit(solution)/shard_map/all_to_all | solution.py:129
  26.0 3.9 %all-gather.3.cloned.1.call-done = bf16[2,512,512]{2,1,0:T(8,128)(2,1)} async-done(((bf16[2,128,512]{2,1,0:T(8,128)(2,1)}), bf16[2,512,512]{2,1,0:T(8,128)(2,1)}) %all-gather.3.cloned.1.call-update) | async-done | bytes 1048592 | tf_op jit(solution)/shard_map/all_gather | solution.py:140
  29.9 1.9 %fusion.26 = bf16[2,128,128]{2,1,0:T(8,128)(2,1)S(1)} fusion(bf16[2,512,512]{2,1,0:T(8,128)(2,1)} %all-gather.3.cloned.1.call-done, bf16[512,128]{1,0:T(8,128)(2,1)S(1)} %maximum_convert_fusion, bf16[512,512]{1,0:T(8,128)(2,1)S(1)} %copy-done.5, s32[]{:T(128)S(6)} %select_n.140), kind=kOutput, calls=%fused_computation.65 | convolution fusion | flops 167936000 | bytes 1376260 | tf_op jit(solution)/shard_map/mxy,yv->mxv/dot_general | solution.py:143
  32.3 10.4 %psum.14 = bf16[2,64,128]{2,1,0:T(8,128)(2,1)S(1)} all-reduce(bf16[2,64,128]{2,1,0:T(8,128)(2,1)S(1)} %pad_maximum_fusion.1), channel_id=1, replica_groups=mesh['ctx'=8,'tile'=4] {'tile'}, use_global_device_ids=true, to_apply=%region_1.2 | all-reduce | flops 16384 | bytes 65536 | tf_op jit(solution)/shard_map/psum | solution.py:147
  42.7 0.3 convolution_convert_fusion.5
  43.0 0.7 copy.79
  43.6 5.7 %all-to-all-start.1 = ((bf16[8,64,128]{2,1,0:T(8,128)(2,1)}), bf16[8,64,128]{2,1,0:T(8,128)(2,1)S(1)}, u32[]{:S(2)}, u32[]{:S(2)}) async-start(bf16[8,64,128]{2,1,0:T(8,128)(2,1)} %copy.79), calls=%async_computation.1 | async-start | bytes 262144 | tf_op jit(solution)/shard_map/all_to_all | solution.py:151
  49.5 7.2 %all-to-all-done.1 = bf16[8,64,128]{2,1,0:T(8,128)(2,1)S(1)} async-done(((bf16[8,64,128]{2,1,0:T(8,128)(2,1)}), bf16[8,64,128]{2,1,0:T(8,128)(2,1)S(1)}, u32[]{:S(2)}, u32[]{:S(2)}) %all-to-all-start.1) | async-done | bytes 131104 | tf_op jit(solution)/shard_map/all_to_all | solution.py:151
  56.7 0.6 gather_fusion
  57.3 0.3 fusion.35
  57.6 4.6 %multiply_subtract_fusion.2 = (f32[24,64,64]{2,0,1:T(8,128)S(1)}, f32[24,64,64]{2,0,1:T(8,128)S(1)}) fusion(f32[24,64,128]{2,0,1:T(8,128)S(1)} %fusion.35, s32[24,64]{1,0:T(8,128)S(1)} %get-tuple-element.289, s32[24,64]{0,1:T(8,128)S(1)} %copy.74), kind=kLoop, calls=%fused_computation.79 | loop fusion | flops 2064384 | bytes 1585152 | tf_op jit(solution)/shard_map/sub | solution.py:64
  62.2 0.3 pad_maximum_fusion
  62.7 0.7 copy-done.4
  63.4 19.3 %while.14 = (s32[]{:T(128)}, bf16[2,128,512]{2,1,0:T(8,128)(2,1)}, bf16[2,64,128]{2,1,0:T(8,128)(2,1)S(1)}, f32[6,64,128]{2,1,0:T(8,128)S(1)}, f32[2,64,128]{2,1...) while((s32[]{:T(128)}, bf16[2,128,512]{2,1,0:T(8,128)(2,1)}, ...), condition=%wide.region_6.7_spmd, body=%wide.region_3.6_spmd.sunk | while | flops 538632192 | bytes 57360672 | solution.py:175
  63.6 0.4 convolution_convert_fusion.9
  64.0 0.6 convolution_bitcast_fusion.11
  64.7 0.6 convolution_bitcast_fusion.12
  65.3 1.0 copy-done.1
  66.3 0.4 add_reduce_fusion.2
  66.8 1.2 copy-done.2
  68.5 3.3 %multiply_convert_fusion.4 = (bf16[6,128,512]{1,2,0:T(8,128)(2,1)S(1)}, bf16[6,128,512]{1,2,0:T(8,128)(2,1)S(1)}) fusion(f32[128,512]{0,1:T(8,128)S(1)} %fusion.130, f32[6,128,1024]{1,2,0:T(8,128)} %copy-done.1, f32[6,128,1024]{1,2,0:T(8,128)} %copy-done.2), kind=kLoop, calls=%fused_computation.10.clone.1 | loop fusion | flops 2359296 | bytes 8126464 | tf_op jit(solution)/shard_map/convert
  71.8 0.6 fusion.131
  73.3 0.4 convolution_convert_fusion.9
  73.7 0.6 convolution_bitcast_fusion.11
  74.4 0.6 convolution_bitcast_fusion.12
  75.0 1.0 copy-done.1
  76.0 0.4 add_reduce_fusion.2
  76.4 1.2 copy-done.2
  78.2 3.3 %multiply_convert_fusion.4 = (bf16[6,128,512]{1,2,0:T(8,128)(2,1)S(1)}, bf16[6,128,512]{1,2,0:T(8,128)(2,1)S(1)}) fusion(f32[128,512]{0,1:T(8,128)S(1)} %fusion.130, f32[6,128,1024]{1,2,0:T(8,128)} %copy-done.1, f32[6,128,1024]{1,2,0:T(8,128)} %copy-done.2), kind=kLoop, calls=%fused_computation.10.clone.1 | loop fusion | flops 2359296 | bytes 8126464 | tf_op jit(solution)/shard_map/convert
  81.5 0.6 fusion.131
  82.8 10.4 %psum.15 = bf16[2,64,128]{2,1,0:T(8,128)(2,1)S(1)} all-reduce(bf16[2,64,128]{2,1,0:T(8,128)(2,1)S(1)} %get-tuple-element.159), channel_id=1, replica_groups=mesh['ctx'=8,'tile'=4] {'tile'}, use_global_device_ids=true, to_apply=%region_7.8 | all-reduce | flops 16384 | bytes 65536 | tf_op jit(solution)/shard_map/psum | solution.py:176
  93.3 0.3 fusion.94
  93.6 3.7 %multiply_subtract_fusion.1 = (f32[24,64,64]{2,0,1:T(8,128)S(1)}, f32[24,64,64]{2,0,1:T(8,128)S(1)}) fusion(f32[24,64,64]{2,1,0:T(8,128)S(1)} %get-tuple-element.276, f32[24,64,64]{2,1,0:T(8,128)S(1)} %get-tuple-element.275, s32[24,64]{1,0:T(8,128)S(1)} %get-tuple-element.289, s32[24,64]{0,1:T(8,128)S(1)} %copy.74), kind=kLoop, calls=%fused_computation.77 | loop fusion | flops 1966080 | bytes 1585152 | tf_op jit(solution)/shard_map/sub | solution.py:64
  97.3 0.5 convolution_convert_fusion.6
  97.8 9.9 %all_to_all.19 = bf16[8,64,128]{2,1,0:T(8,128)(2,1)S(1)} all-to-all(bf16[8,64,128]{2,1,0:T(8,128)(2,1)S(1)} %copy.87), channel_id=1, replica_groups=mesh['ctx'=8,'tile'=4] {'ctx'}, dimensions={0} | all-to-all | bytes 262144 | tf_op jit(solution)/shard_map/all_to_all | solution.py:185
  108.5 1.3 %convolution_convert_fusion.1 = bf16[2,128,512]{2,1,0:T(8,128)(2,1)} fusion(f32[2,512,128]{2,1,0:T(8,128)S(1)} %fusion.52, bf16[512,512]{1,0:T(8,128)(2,1)S(1)} %copy-done, bf16[2,64,1024]{2,1,0:T(8,128)(2,1)S(1)} %convolution_convert_fusion.2, bf16[128,64]{1,0:T(8,128)(2,1)S(1)} %constant_dynamic-slice_fusion.1), kind=kOutput, calls=%fused_computation.54 | convolution fusion | flops 151388160 | bytes 1474560 | tf_op jit(solution)/shard_map/mxy,yz->mxz/dot_general | solution.py:202
  109.8 14.5 %all-gather.5.cloned.1.call-done = bf16[2,512,512]{2,1,0:T(8,128)(2,1)} async-done(((bf16[2,128,512]{2,1,0:T(8,128)(2,1)}), bf16[2,512,512]{2,1,0:T(8,128)(2,1)}) %all-gather.5.cloned.1.call-update) | async-done | bytes 1048592 | tf_op jit(solution)/shard_map/all_gather | solution.py:209
  124.3 1.7 %convolution_bitcast_fusion.4 = f32[2,128,512]{1,2,0:T(8,128)S(1)} fusion(bf16[2,512,512]{2,1,0:T(8,128)(2,1)} %all-gather.5.cloned.1.call-done, bf16[512,512]{1,0:T(8,128)(2,1)S(1)} %copy-done.5, s32[]{:T(128)S(6)} %select_n.140), kind=kOutput, calls=%fused_computation.51 | convolution fusion | flops 134217728 | bytes 1703940 | tf_op jit(solution)/shard_map/jx,mjz->mxz/dot_general | solution.py:206
  126.0 1.0 copy.95
  (82 shorter events, 5.6 us)
Async XLA Ops:
  7.2 1.0 copy-start
  7.2 22.7 %all-gather.3.cloned.1.call-start = ((), (), s32[]{:S(2)}) async-start(), calls=%async_computation.3 | async-start | bytes 1310720 | tf_op jit(solution)/shard_map/all_gather | solution.py:140
  10.2 19.7 %copy-start.5 = (bf16[512,512]{1,0:T(8,128)(2,1)S(1)}, bf16[512,512]{1,0:T(8,128)(2,1)}, u32[]{:S(2)}) copy-start(bf16[512,512]{1,0:T(8,128)(2,1)} %param.10) | copy-start | bytes 1572868
  11.9 13.8 %all-to-all-start = ((s32[8,1,1]{2,1,0:T(1,128)}), s32[8,1,1]{2,1,0:T(1,128)S(1)}, u32[]{:S(2)}, u32[]{:S(2)}) async-start(s32[8,1,1]{2,1,0:T(1,128)} %copy.75), calls=%async_computation | async-start | bytes 8192 | tf_op jit(solution)/shard_map/all_to_all | solution.py:129
  23.6 25.8 %copy-start.3 = (f32[6,64,128]{2,1,0:T(8,128)S(1)}, f32[6,64,128]{2,1,0:T(8,128)}, u32[]{:S(2)}) copy-start(f32[6,64,128]{2,1,0:T(8,128)} %param.12) | copy-start | bytes 589828
  43.6 13.0 %all-to-all-start.1 = ((bf16[8,64,128]{2,1,0:T(8,128)(2,1)}), bf16[8,64,128]{2,1,0:T(8,128)(2,1)S(1)}, u32[]{:S(2)}, u32[]{:S(2)}) async-start(bf16[8,64,128]{2,1,0:T(8,128)(2,1)} %copy.79), calls=%async_computation.1 | async-start | bytes 262144 | tf_op jit(solution)/shard_map/all_to_all | solution.py:151
  49.3 75.0 %all-gather.5.cloned.1.call-start = ((), (), s32[]{:S(2)}) async-start(), calls=%async_computation.4 | async-start | bytes 1310720 | tf_op jit(solution)/shard_map/all_gather | solution.py:209
  62.5 1.0 copy-start.4
  64.7 1.6 %copy-start.1 = (f32[6,128,1024]{1,2,0:T(8,128)}, f32[6,128,1024]{1,2,0:T(8,128)S(1)}, u32[]{:S(2)}) copy-start(f32[6,128,1024]{1,2,0:T(8,128)S(1)} %convolution_bitcast_fusion.11) | copy-start | bytes 9437188 | tf_op jit(solution)/shard_map/while
  66.3 1.7 %copy-start.2 = (f32[6,128,1024]{1,2,0:T(8,128)}, f32[6,128,1024]{1,2,0:T(8,128)S(1)}, u32[]{:S(2)}) copy-start(f32[6,128,1024]{1,2,0:T(8,128)S(1)} %convolution_bitcast_fusion.12) | copy-start | bytes 9437188 | tf_op jit(solution)/shard_map/while
  66.3 1.9 %copy-start.6 = (bf16[2,128,512]{2,1,0:T(8,128)(2,1)S(1)}, bf16[2,128,512]{2,1,0:T(8,128)(2,1)}, u32[]{:S(2)}) copy-start(bf16[2,128,512]{2,1,0:T(8,128)(2,1)} %get-tuple-element.410) | copy-start | bytes 786436 | tf_op jit(solution)/shard_map/while
  68.2 3.6 %copy-start.7 = (bf16[2,128,512]{2,1,0:T(8,128)(2,1)}, bf16[2,128,512]{2,1,0:T(8,128)(2,1)S(1)}, u32[]{:S(2)}) copy-start(bf16[2,128,512]{2,1,0:T(8,128)(2,1)S(1)} %get-tuple-element.426) | copy-start | bytes 786436 | tf_op jit(solution)/shard_map/while
  74.4 1.6 %copy-start.1 = (f32[6,128,1024]{1,2,0:T(8,128)}, f32[6,128,1024]{1,2,0:T(8,128)S(1)}, u32[]{:S(2)}) copy-start(f32[6,128,1024]{1,2,0:T(8,128)S(1)} %convolution_bitcast_fusion.11) | copy-start | bytes 9437188 | tf_op jit(solution)/shard_map/while
  76.0 1.7 %copy-start.2 = (f32[6,128,1024]{1,2,0:T(8,128)}, f32[6,128,1024]{1,2,0:T(8,128)S(1)}, u32[]{:S(2)}) copy-start(f32[6,128,1024]{1,2,0:T(8,128)S(1)} %convolution_bitcast_fusion.12) | copy-start | bytes 9437188 | tf_op jit(solution)/shard_map/while
  76.0 1.9 %copy-start.6 = (bf16[2,128,512]{2,1,0:T(8,128)(2,1)S(1)}, bf16[2,128,512]{2,1,0:T(8,128)(2,1)}, u32[]{:S(2)}) copy-start(bf16[2,128,512]{2,1,0:T(8,128)(2,1)} %get-tuple-element.410) | copy-start | bytes 786436 | tf_op jit(solution)/shard_map/while
  77.9 3.6 %copy-start.7 = (bf16[2,128,512]{2,1,0:T(8,128)(2,1)}, bf16[2,128,512]{2,1,0:T(8,128)(2,1)S(1)}, u32[]{:S(2)}) copy-start(bf16[2,128,512]{2,1,0:T(8,128)(2,1)S(1)} %get-tuple-element.426) | copy-start | bytes 786436 | tf_op jit(solution)/shard_map/while
Sparse Core Ops, SparseCore 0:
  10.3 19.4 all-gather.2
  110.0 14.2 all-gather.4
where the time goes:
time: 134 us
  blocking collectives  30.8 us (23%)
  waiting for transfers between devices  27.6 us (21%)
  other arithmetic  22.2 us (17%)
  between operations  14.3 us (11%)
  matrix products  13.9 us (10%)
  starting transfers between devices  13.1 us (10%)
  local copies, waits for them, and re-layouts  11.7 us (9%)
    all_gather x1, waiting for transfers between devices, local(): lax.all_gather(settled, 'tile', axis=1, tiled=True)  14.5 us
    psum x1, blocking collectives, local(): lax.psum(grad_part.astype(jnp.bfloat16), 'tile').astype(jnp.float32)  10.4 us
    psum x1, blocking collectives, local(): spectra = lax.psum(partial_value.astype(jnp.bfloat16), 'tile')  10.4 us
    all_to_all x1, blocking collectives, local(): lax.all_to_all(returned.astype(jnp.bfloat16), 'ctx', split_axis=0, concat...  9.92 us
    sub x4, other arithmetic, complex_times(): factor_real * values_real - factor_imag * values_imag  8.65 us
    another operation x6, other arithmetic  7.55 us
    all_to_all x1, starting transfers between devices, local(): lax.all_to_all(wanted[:, None], 'ctx', split_axis=0, concat_axis=0, tiled...  7.31 us
    all_to_all x1, waiting for transfers between devices, local(): lax.all_to_all(outgoing, 'ctx', split_axis=0, concat_axis=0, tiled=True)  7.17 us
  transfers between devices with their start and end apart: 4, of which 4 were waited for; matrix products, arithmetic and copies ran while one was open for 5% of the time, Pallas kernels for 0%

commit v1 on v0

--- a/solution.py
+++ b/solution.py
@@ -173,7 +173,9 @@
         )
 
     resist, grad_part = lax.map(one_context, (context_spec, targets))
-    grad_ctx = lax.psum(grad_part.astype(jnp.bfloat16), "tile").astype(jnp.float32)
+    grad_ctx = jnp.sum(lax.all_gather(grad_part.astype(jnp.bfloat16), "tile"), axis=0).astype(
+        jnp.float32
+    )
     band_start = 0
     repeated = jnp.repeat(grad_ctx, source_count, axis=0)
     back_turn = complex_times(

time: 134 us -> 130 us (0.970)
  blocking collectives: 30.8 us -> 26.1 us
    psum x1 -> x0, blocking collectives: 10.4 us -> none  [local(): lax.psum(grad_part.astype(jnp.bfloat16), 'tile').astype(jnp.float32)]
    all_gather x0 -> x1, blocking collectives: none -> 5.6 us  [local(): lax.all_gather(grad_part.astype(jnp.bfloat16), 'tile')]
where the time goes in v1:
time: 130 us
  waiting for transfers between devices  28.1 us (22%)
  blocking collectives  26.1 us (20%)
  other arithmetic  22.2 us (17%)
  between operations  14.3 us (11%)
  matrix products  13.9 us (11%)
  starting transfers between devices  13.1 us (10%)
  local copies, waits for them, and re-layouts  11.7 us (9%)
    all_gather x1, waiting for transfers between devices, local(): lax.all_gather(settled, 'tile', axis=1, tiled=True)  15 us
    psum x1, blocking collectives, local(): spectra = lax.psum(partial_value.astype(jnp.bfloat16), 'tile')  10.4 us
    all_to_all x1, blocking collectives, local(): lax.all_to_all(returned.astype(jnp.bfloat16), 'ctx', split_axis=0, concat...  10.2 us
    sub x4, other arithmetic, complex_times(): factor_real * values_real - factor_imag * values_imag  8.65 us
    another operation x6, other arithmetic  7.55 us
    all_to_all x1, starting transfers between devices, local(): lax.all_to_all(wanted[:, None], 'ctx', split_axis=0, concat_axis=0, tiled...  7.31 us
    all_to_all x1, waiting for transfers between devices, local(): lax.all_to_all(outgoing, 'ctx', split_axis=0, concat_axis=0, tiled=True)  7.17 us
    all_to_all x1, starting transfers between devices, local(): lax.all_to_all(outgoing, 'ctx', split_axis=0, concat_axis=0, tiled=True)  5.67 us
  transfers between devices with their start and end apart: 4, of which 4 were waited for; matrix products, arithmetic and copies ran while one was open for 5% of the time, Pallas kernels for 0%

profile of v1, /device:TPU:0, one launch (start us, length us, event | category | flops | bytes accessed | tf_op | source)
XLA Modules:
  0.0 129.7 jit_solution(12253264693569903342)
XLA Ops:
  7.2 1.0 copy-done
  8.2 2.0 %convolution_convert_fusion.4 = bf16[2,128,512]{2,1,0:T(8,128)(2,1)} fusion(bf16[2,128,512]{2,1,0:T(8,128)(2,1)} %param.9, bf16[512,512]{1,0:T(8,128)(2,1)S(1)} %copy-done), kind=kOutput, calls=%fused_computation.57 | convolution fusion | flops 134348800 | bytes 1048576 | tf_op jit(solution)/shard_map/mxy,zy->mxz/dot_general | solution.py:133
  10.2 0.7 and_select_fusion.1
  11.3 0.7 copy.74
  11.9 7.3 %all-to-all-start = ((s32[8,1,1]{2,1,0:T(1,128)}), s32[8,1,1]{2,1,0:T(1,128)S(1)}, u32[]{:S(2)}, u32[]{:S(2)}) async-start(s32[8,1,1]{2,1,0:T(1,128)} %copy.74), calls=%async_computation | async-start | bytes 8192 | tf_op jit(solution)/shard_map/all_to_all | solution.py:129
  19.3 0.7 copy.72
  20.1 1.1 fusion.45
  21.6 0.6 fusion.65
  22.2 1.1 cosine_multiply_fusion
  23.7 2.0 %all-to-all-done = s32[8,1,1]{2,1,0:T(1,128)S(1)} async-done(((s32[8,1,1]{2,1,0:T(1,128)}), s32[8,1,1]{2,1,0:T(1,128)S(1)}, u32[]{:S(2)}, u32[]{:S(2)}) %all-to-all-start) | async-done | bytes 64 | tf_op jit(solution)/shard_map/all_to_all | solution.py:129
  26.0 3.9 %all-gather.4.cloned.1.call-done = bf16[2,512,512]{2,1,0:T(8,128)(2,1)} async-done(((bf16[2,128,512]{2,1,0:T(8,128)(2,1)}), bf16[2,512,512]{2,1,0:T(8,128)(2,1)}) %all-gather.4.cloned.1.call-update) | async-done | bytes 1048592 | tf_op jit(solution)/shard_map/all_gather | solution.py:140
  29.9 1.9 %fusion.26 = bf16[2,128,128]{2,1,0:T(8,128)(2,1)S(1)} fusion(bf16[2,512,512]{2,1,0:T(8,128)(2,1)} %all-gather.4.cloned.1.call-done, bf16[512,128]{1,0:T(8,128)(2,1)S(1)} %maximum_convert_fusion, bf16[512,512]{1,0:T(8,128)(2,1)S(1)} %copy-done.5, s32[]{:T(128)S(6)} %select_n.140), kind=kOutput, calls=%fused_computation.65 | convolution fusion | flops 167936000 | bytes 1376260 | tf_op jit(solution)/shard_map/mxy,yv->mxv/dot_general | solution.py:143
  32.3 10.4 %psum.7 = bf16[2,64,128]{2,1,0:T(8,128)(2,1)S(1)} all-reduce(bf16[2,64,128]{2,1,0:T(8,128)(2,1)S(1)} %pad_maximum_fusion.1), channel_id=1, replica_groups=mesh['ctx'=8,'tile'=4] {'tile'}, use_global_device_ids=true, to_apply=%region_1.2 | all-reduce | flops 16384 | bytes 65536 | tf_op jit(solution)/shard_map/psum | solution.py:147
  42.7 0.3 convolution_convert_fusion.5
  43.0 0.7 copy.78
  43.6 5.7 %all-to-all-start.1 = ((bf16[8,64,128]{2,1,0:T(8,128)(2,1)}), bf16[8,64,128]{2,1,0:T(8,128)(2,1)S(1)}, u32[]{:S(2)}, u32[]{:S(2)}) async-start(bf16[8,64,128]{2,1,0:T(8,128)(2,1)} %copy.78), calls=%async_computation.1 | async-start | bytes 262144 | tf_op jit(solution)/shard_map/all_to_all | solution.py:151
  49.5 7.2 %all-to-all-done.1 = bf16[8,64,128]{2,1,0:T(8,128)(2,1)S(1)} async-done(((bf16[8,64,128]{2,1,0:T(8,128)(2,1)}), bf16[8,64,128]{2,1,0:T(8,128)(2,1)S(1)}, u32[]{:S(2)}, u32[]{:S(2)}) %all-to-all-start.1) | async-done | bytes 131104 | tf_op jit(solution)/shard_map/all_to_all | solution.py:151
  56.7 0.6 gather_fusion
  57.3 0.3 fusion.35
  57.6 4.6 %multiply_subtract_fusion.2 = (f32[24,64,64]{2,0,1:T(8,128)S(1)}, f32[24,64,64]{2,0,1:T(8,128)S(1)}) fusion(f32[24,64,128]{2,0,1:T(8,128)S(1)} %fusion.35, s32[24,64]{1,0:T(8,128)S(1)} %get-tuple-element.289, s32[24,64]{0,1:T(8,128)S(1)} %copy.73), kind=kLoop, calls=%fused_computation.79 | loop fusion | flops 2064384 | bytes 1585152 | tf_op jit(solution)/shard_map/sub | solution.py:64
  62.2 0.3 pad_maximum_fusion
  62.7 0.7 copy-done.4
  63.4 19.3 %while.14 = (s32[]{:T(128)}, bf16[2,128,512]{2,1,0:T(8,128)(2,1)}, bf16[2,64,128]{2,1,0:T(8,128)(2,1)S(1)}, f32[6,64,128]{2,1,0:T(8,128)S(1)}, f32[2,64,128]{2,1...) while((s32[]{:T(128)}, bf16[2,128,512]{2,1,0:T(8,128)(2,1)}, ...), condition=%wide.region_6.7_spmd, body=%wide.region_3.6_spmd.sunk | while | flops 538632192 | bytes 57360672 | solution.py:175
  63.6 0.4 convolution_convert_fusion.9
  64.0 0.6 convolution_bitcast_fusion.11
  64.7 0.6 convolution_bitcast_fusion.12
  65.3 1.0 copy-done.1
  66.3 0.4 add_reduce_fusion.2
  66.8 1.2 copy-done.2
  68.5 3.3 %multiply_convert_fusion.4 = (bf16[6,128,512]{1,2,0:T(8,128)(2,1)S(1)}, bf16[6,128,512]{1,2,0:T(8,128)(2,1)S(1)}) fusion(f32[128,512]{0,1:T(8,128)S(1)} %fusion.130, f32[6,128,1024]{1,2,0:T(8,128)} %copy-done.1, f32[6,128,1024]{1,2,0:T(8,128)} %copy-done.2), kind=kLoop, calls=%fused_computation.10.clone.1 | loop fusion | flops 2359296 | bytes 8126464 | tf_op jit(solution)/shard_map/convert.1
  71.8 0.6 fusion.131
  73.3 0.4 convolution_convert_fusion.9
  73.7 0.6 convolution_bitcast_fusion.11
  74.4 0.6 convolution_bitcast_fusion.12
  75.0 1.0 copy-done.1
  76.0 0.4 add_reduce_fusion.2
  76.4 1.2 copy-done.2
  78.2 3.3 %multiply_convert_fusion.4 = (bf16[6,128,512]{1,2,0:T(8,128)(2,1)S(1)}, bf16[6,128,512]{1,2,0:T(8,128)(2,1)S(1)}) fusion(f32[128,512]{0,1:T(8,128)S(1)} %fusion.130, f32[6,128,1024]{1,2,0:T(8,128)} %copy-done.1, f32[6,128,1024]{1,2,0:T(8,128)} %copy-done.2), kind=kLoop, calls=%fused_computation.10.clone.1 | loop fusion | flops 2359296 | bytes 8126464 | tf_op jit(solution)/shard_map/convert.1
  81.5 0.6 fusion.131
  82.8 5.6 %all-gather = bf16[8,64,128]{2,1,0:T(8,128)(2,1)S(1)} all-gather(bf16[2,64,128]{2,1,0:T(8,128)(2,1)S(1)} %get-tuple-element.159), channel_id=2, replica_groups=mesh['ctx'=8,'tile'=4] {'tile'}, dimensions={0}, use_global_device_ids=true | all-gather | bytes 163840 | tf_op jit(solution)/shard_map/all_gather | solution.py:176
  88.5 0.3 fusion.94
  88.8 3.7 %multiply_subtract_fusion.1 = (f32[24,64,64]{2,0,1:T(8,128)S(1)}, f32[24,64,64]{2,0,1:T(8,128)S(1)}) fusion(f32[24,64,64]{2,1,0:T(8,128)S(1)} %get-tuple-element.276, f32[24,64,64]{2,1,0:T(8,128)S(1)} %get-tuple-element.275, s32[24,64]{1,0:T(8,128)S(1)} %get-tuple-element.289, s32[24,64]{0,1:T(8,128)S(1)} %copy.73), kind=kLoop, calls=%fused_computation.77 | loop fusion | flops 1966080 | bytes 1585152 | tf_op jit(solution)/shard_map/sub | solution.py:64
  92.4 0.5 convolution_convert_fusion.6
  93.0 10.2 %all_to_all.19 = bf16[8,64,128]{2,1,0:T(8,128)(2,1)S(1)} all-to-all(bf16[8,64,128]{2,1,0:T(8,128)(2,1)S(1)} %copy.86), channel_id=1, replica_groups=mesh['ctx'=8,'tile'=4] {'ctx'}, dimensions={0} | all-to-all | bytes 262144 | tf_op jit(solution)/shard_map/all_to_all | solution.py:187
  103.9 1.3 %convolution_convert_fusion.1 = bf16[2,128,512]{2,1,0:T(8,128)(2,1)} fusion(f32[2,512,128]{2,1,0:T(8,128)S(1)} %fusion.52, bf16[512,512]{1,0:T(8,128)(2,1)S(1)} %copy-done, bf16[2,64,1024]{2,1,0:T(8,128)(2,1)S(1)} %convolution_convert_fusion.2, bf16[128,64]{1,0:T(8,128)(2,1)S(1)} %constant_dynamic-slice_fusion.1), kind=kOutput, calls=%fused_computation.54 | convolution fusion | flops 151388160 | bytes 1474560 | tf_op jit(solution)/shard_map/mxy,yz->mxz/dot_general | solution.py:204
  105.2 15.0 %all-gather.6.cloned.1.call-done = bf16[2,512,512]{2,1,0:T(8,128)(2,1)} async-done(((bf16[2,128,512]{2,1,0:T(8,128)(2,1)}), bf16[2,512,512]{2,1,0:T(8,128)(2,1)}) %all-gather.6.cloned.1.call-update) | async-done | bytes 1048592 | tf_op jit(solution)/shard_map/all_gather | solution.py:211
  120.2 1.7 %convolution_bitcast_fusion.4 = f32[2,128,512]{1,2,0:T(8,128)S(1)} fusion(bf16[2,512,512]{2,1,0:T(8,128)(2,1)} %all-gather.6.cloned.1.call-done, bf16[512,512]{1,0:T(8,128)(2,1)S(1)} %copy-done.5, s32[]{:T(128)S(6)} %select_n.140), kind=kOutput, calls=%fused_computation.51 | convolution fusion | flops 134217728 | bytes 1703940 | tf_op jit(solution)/shard_map/jx,mjz->mxz/dot_general | solution.py:208
  121.9 1.0 copy.94
  (83 shorter events, 5.7 us)
Async XLA Ops:
  7.2 1.0 copy-start
  7.2 22.7 %all-gather.4.cloned.1.call-start = ((), (), s32[]{:S(2)}) async-start(), calls=%async_computation.3 | async-start | bytes 1310720 | tf_op jit(solution)/shard_map/all_gather | solution.py:140
  10.2 19.7 %copy-start.5 = (bf16[512,512]{1,0:T(8,128)(2,1)S(1)}, bf16[512,512]{1,0:T(8,128)(2,1)}, u32[]{:S(2)}) copy-start(bf16[512,512]{1,0:T(8,128)(2,1)} %param.10) | copy-start | bytes 1572868
  11.9 13.8 %all-to-all-start = ((s32[8,1,1]{2,1,0:T(1,128)}), s32[8,1,1]{2,1,0:T(1,128)S(1)}, u32[]{:S(2)}, u32[]{:S(2)}) async-start(s32[8,1,1]{2,1,0:T(1,128)} %copy.74), calls=%async_computation | async-start | bytes 8192 | tf_op jit(solution)/shard_map/all_to_all | solution.py:129
  23.6 25.8 %copy-start.3 = (f32[6,64,128]{2,1,0:T(8,128)S(1)}, f32[6,64,128]{2,1,0:T(8,128)}, u32[]{:S(2)}) copy-start(f32[6,64,128]{2,1,0:T(8,128)} %param.12) | copy-start | bytes 589828
  43.6 13.0 %all-to-all-start.1 = ((bf16[8,64,128]{2,1,0:T(8,128)(2,1)}), bf16[8,64,128]{2,1,0:T(8,128)(2,1)S(1)}, u32[]{:S(2)}, u32[]{:S(2)}) async-start(bf16[8,64,128]{2,1,0:T(8,128)(2,1)} %copy.78), calls=%async_computation.1 | async-start | bytes 262144 | tf_op jit(solution)/shard_map/all_to_all | solution.py:151
  49.3 70.9 %all-gather.6.cloned.1.call-start = ((), (), s32[]{:S(2)}) async-start(), calls=%async_computation.4 | async-start | bytes 1310720 | tf_op jit(solution)/shard_map/all_gather | solution.py:211
  62.5 1.0 copy-start.4
  64.7 1.6 %copy-start.1 = (f32[6,128,1024]{1,2,0:T(8,128)}, f32[6,128,1024]{1,2,0:T(8,128)S(1)}, u32[]{:S(2)}) copy-start(f32[6,128,1024]{1,2,0:T(8,128)S(1)} %convolution_bitcast_fusion.11) | copy-start | bytes 9437188 | tf_op jit(solution)/shard_map/while
  66.3 1.7 %copy-start.2 = (f32[6,128,1024]{1,2,0:T(8,128)}, f32[6,128,1024]{1,2,0:T(8,128)S(1)}, u32[]{:S(2)}) copy-start(f32[6,128,1024]{1,2,0:T(8,128)S(1)} %convolution_bitcast_fusion.12) | copy-start | bytes 9437188 | tf_op jit(solution)/shard_map/while
  66.3 1.9 %copy-start.6 = (bf16[2,128,512]{2,1,0:T(8,128)(2,1)S(1)}, bf16[2,128,512]{2,1,0:T(8,128)(2,1)}, u32[]{:S(2)}) copy-start(bf16[2,128,512]{2,1,0:T(8,128)(2,1)} %get-tuple-element.410) | copy-start | bytes 786436 | tf_op jit(solution)/shard_map/while
  68.2 3.6 %copy-start.7 = (bf16[2,128,512]{2,1,0:T(8,128)(2,1)}, bf16[2,128,512]{2,1,0:T(8,128)(2,1)S(1)}, u32[]{:S(2)}) copy-start(bf16[2,128,512]{2,1,0:T(8,128)(2,1)S(1)} %get-tuple-element.426) | copy-start | bytes 786436 | tf_op jit(solution)/shard_map/while
  74.4 1.6 %copy-start.1 = (f32[6,128,1024]{1,2,0:T(8,128)}, f32[6,128,1024]{1,2,0:T(8,128)S(1)}, u32[]{:S(2)}) copy-start(f32[6,128,1024]{1,2,0:T(8,128)S(1)} %convolution_bitcast_fusion.11) | copy-start | bytes 9437188 | tf_op jit(solution)/shard_map/while
  76.0 1.7 %copy-start.2 = (f32[6,128,1024]{1,2,0:T(8,128)}, f32[6,128,1024]{1,2,0:T(8,128)S(1)}, u32[]{:S(2)}) copy-start(f32[6,128,1024]{1,2,0:T(8,128)S(1)} %convolution_bitcast_fusion.12) | copy-start | bytes 9437188 | tf_op jit(solution)/shard_map/while
  76.0 1.9 %copy-start.6 = (bf16[2,128,512]{2,1,0:T(8,128)(2,1)S(1)}, bf16[2,128,512]{2,1,0:T(8,128)(2,1)}, u32[]{:S(2)}) copy-start(bf16[2,128,512]{2,1,0:T(8,128)(2,1)} %get-tuple-element.410) | copy-start | bytes 786436 | tf_op jit(solution)/shard_map/while
  77.9 3.6 %copy-start.7 = (bf16[2,128,512]{2,1,0:T(8,128)(2,1)}, bf16[2,128,512]{2,1,0:T(8,128)(2,1)S(1)}, u32[]{:S(2)}) copy-start(bf16[2,128,512]{2,1,0:T(8,128)(2,1)S(1)} %get-tuple-element.426) | copy-start | bytes 786436 | tf_op jit(solution)/shard_map/while
Sparse Core Ops, SparseCore 0:
  10.3 19.4 all-gather.3
  105.4 14.7 all-gather.5
